TPU v7x, 32 devices: a whole 2x2x4 slice. The times are simulated.
32 devices in a mesh: seq: 8 (over z, y), batch: 4 (over x, core).
Axes of the slice: x: 2, y: 2, z: 4, core: 2. Of those that a mesh axis runs over, the one named last changes fastest.
Arguments:
- conv_input: bfloat16 [4096, 8192], P(('batch', 'seq')), parts along dimension 0, may hold values from -6 to 6
- gate_input: bfloat16 [4096, 8192], P(('batch', 'seq')), parts along dimension 0, may hold values from -6 to 6
- conv_weight: bfloat16 [4, 8192], P(None, 'seq'), may hold values from -3 to 3
- conv_bias: bfloat16 [8192], P('seq'), may hold values from -3 to 3
- x_weight: bfloat16 [8192, 288], P('seq'), may hold values from -0.0625 to 0.0625
- dt_gain: float32 [256], replicated, may hold values from 0.5 to 1.5
- dt_weight: bfloat16 [256, 8192], P(None, 'seq'), may hold values from -0.375 to 0.375
- dt_bias: float32 [8192], P('seq'), may hold values from -6.9 to -2.3
- a_log: float32 [16, 8192], P(None, 'seq'), may hold values from 0 to 2.77
- skip: float32 [8192], P('seq'), may hold values from 0.5 to 1.5
Outputs:
- mixed: bfloat16 [4096, 8192], P(('batch', 'seq')), parts along dimension 0
There are 4 independent parts, one for each index of `batch`. A program takes and returns all parts, laid end to end along the dimension named above; an argument that names none is the same for every part. Nothing has to cross between parts.
All inputs are finite; a program needn't handle non-finite values.
Results may differ from a plain program's by a relative error of at most 0.0085.
Values may be sent and summed in bfloat16 or wider, within the bound.
A program may use at most 128 MiB of HBM per device.

v0:
```python
import jax
import jax.numpy as jnp
from jax import lax
from jax.sharding import PartitionSpec as P


def causal_conv(prefix, inputs, weight, bias):
    rows = inputs.shape[0]
    width = weight.shape[0]
    padded = jnp.concatenate([prefix, inputs.astype(jnp.float32)], 0)
    total = bias.astype(jnp.float32)[None, :]
    for tap in range(width):
        total = total + weight[tap].astype(jnp.float32)[None, :] * padded[tap : tap + rows]
    return jax.nn.silu(total).astype(jnp.bfloat16)


def link_blocks(earlier, later):
    return (earlier[0] * later[0], later[0] * earlier[1] + later[1])


def selective_scan(step, xfloat, bmat, cmat, rate):
    span = 16
    length, chans = step.shape
    states = rate.shape[0]
    blocks = length // span
    step_rows = step.reshape(blocks, span * chans)
    drive_rows = (step * xfloat).reshape(blocks, span * chans)
    b_rows = bmat.reshape(blocks, span * states)
    c_rows = cmat.reshape(blocks, span * states)
    state = jnp.zeros((blocks, states, chans), jnp.float32)
    running = jnp.zeros((blocks, chans), jnp.float32)
    local_parts = []
    elapsed = []
    for place in range(span):
        step_now = step_rows[:, place * chans : (place + 1) * chans]
        drive_now = drive_rows[:, place * chans : (place + 1) * chans]
        b_now = b_rows[:, place * states : (place + 1) * states]
        c_now = c_rows[:, place * states : (place + 1) * states]
        state = (
            jnp.exp(step_now[:, None, :] * rate[None]) * state
            + b_now[:, :, None] * drive_now[:, None, :]
        )
        local_parts.append(jnp.sum(c_now[:, :, None] * state, axis=1))
        running = running + step_now
        elapsed.append(running)
    totals = jnp.exp(running[:, None, :] * rate[None])
    _, through = lax.associative_scan(link_blocks, (totals, state), axis=0)
    starts = jnp.concatenate([jnp.zeros((1, states, chans), jnp.float32), through[: blocks - 1]], 0)
    pieces = []
    for place in range(span):
        c_now = c_rows[:, place * states : (place + 1) * states]
        carried = jnp.sum(
            c_now[:, :, None] * jnp.exp(elapsed[place][:, None, :] * rate[None]) * starts, axis=1
        )
        pieces.append(local_parts[place] + carried)
    return jnp.concatenate(pieces, 1).reshape(length, chans)


def local(
    conv_input,
    gate_input,
    conv_weight,
    conv_bias,
    x_weight,
    dt_gain,
    dt_weight,
    dt_bias,
    a_log,
    skip,
):
    width = conv_weight.shape[0]
    rank = dt_weight.shape[0]
    states = a_log.shape[0]
    arrived = lax.all_to_all(conv_input, "seq", split_axis=1, concat_axis=0, tiled=True)
    zero_prefix = jnp.zeros((width - 1, arrived.shape[1]), jnp.float32)
    conv_out = causal_conv(zero_prefix, arrived, conv_weight, conv_bias)
    partial_value = jnp.dot(conv_out, x_weight, preferred_element_type=jnp.float32)
    proj = lax.psum(partial_value, "seq")
    dt_low = proj[:, :rank]
    bmat = proj[:, rank : rank + states]
    cmat = proj[:, rank + states :]
    normed = (
        dt_low
        * lax.rsqrt(jnp.mean(dt_low * dt_low, axis=1, keepdims=True) + 1e-06)
        * dt_gain[None, :]
    ).astype(jnp.bfloat16)
    step = jax.nn.softplus(
        jnp.dot(normed, dt_weight, preferred_element_type=jnp.float32) + dt_bias[None, :]
    )
    rate = -jnp.exp(a_log)
    xfloat = conv_out.astype(jnp.float32)
    scanned = selective_scan(step, xfloat, bmat, cmat, rate)
    y_out = (scanned + skip[None, :] * xfloat).astype(jnp.bfloat16)
    returned = lax.all_to_all(y_out, "seq", split_axis=0, concat_axis=1, tiled=True)
    return (returned.astype(jnp.float32) * jax.nn.silu(gate_input.astype(jnp.float32))).astype(
        jnp.bfloat16
    )


def solution(mesh):
    return jax.shard_map(
        local,
        mesh=mesh,
        in_specs=(
            P(("batch", "seq"), None),
            P(("batch", "seq"), None),
            P(None, "seq"),
            P("seq"),
            P("seq", None),
            P(),
            P(None, "seq"),
            P("seq"),
            P(None, "seq"),
            P("seq"),
        ),
        out_specs=P(("batch", "seq"), None),
        check_vma=False,
    )
```

profile of v0, /device:TPU:0, one launch (start us, length us, event | category | flops | bytes accessed | tf_op | source)
XLA Modules:
  0.0 461.8 jit_solution(15684360439202959962)
XLA Ops:
  6.5 3.2 copy.24
  9.8 7.3 %all-to-all-start = ((bf16[128,8,1024]{2,0,1:T(8,128)(2,1)}), bf16[128,8,1024]{2,0,1:T(8,128)(2,1)S(1)}, u32[]{:S(2)}, u32[]{:S(2)}) async-start(bf16[128,8,1024]{2,0,1:T(8,128)(2,1)} %bitcast.22), calls=%async_computation | async-start | bytes 4194304 | tf_op jit(solution)/shard_map/all_to_all | solution.py:74
  17.2 48.1 %all-to-all-done = bf16[128,8,1024]{2,0,1:T(8,128)(2,1)S(1)} async-done(((bf16[128,8,1024]{2,0,1:T(8,128)(2,1)}), bf16[128,8,1024]{2,0,1:T(8,128)(2,1)S(1)}, u32[]{:S(2)}, u32[]{:S(2)}) %all-to-all-start) | async-done | bytes 2097184 | tf_op jit(solution)/shard_map/all_to_all | solution.py:74
  65.8 1.9 copy-done.2
  67.7 2.7 multiply_convert_fusion
  70.5 1.8 fusion.27
  72.4 79.5 %all-reduce.16.cloned.1.call-done = f32[1024,288]{0,1:T(8,128)} async-done(((f32[1024,288]{0,1:T(8,128)}), f32[1024,288]{0,1:T(8,128)}) %all-reduce.16.cloned.1.call-update) | async-done | bytes 1179664 | tf_op jit(solution)/shard_map/psum | solution.py:78
  151.9 1.3 multiply_reduce_fusion.32
  153.3 7.3 %convert_multiply_fusion.2 = (f32[1024,1024]{1,0:T(8,128)}, f32[1024,1024]{1,0:T(8,128)}) fusion(bf16[1024,1024]{1,0:T(8,128)(2,1)S(1)} %multiply_convert_fusion, f32[1024]{0:T(1024)S(1)} %copy-done.125, bf16[256,1024]{1,0:T(8,128)(2,1)S(1)} %copy-done.124, f32[1024,288]{0,1:T(8,128)} %all-reduce.16.cloned.1.call-done, f32[256]{0:T(256)S(1)} %copy-done.126, ...), kind=kOutput, calls=%fused_computation.4 | convolution fusion | flops 547094528 | bytes 12067840 | tf_op jit(solution)/shard_map/dot_general | solution.py:88
  160.6 5.0 %reshape.118 = f32[64,16384]{1,0:T(8,128)} reshape(f32[1024,1024]{1,0:T(8,128)} %get-tuple-element.143) | data formatting | bytes 8388608 | tf_op jit(solution)/shard_map/reshape | solution.py:26
  165.6 3.4 fusion.19
  169.3 2.1 slice_add_fusion.20
  171.4 1.0 fusion.21
  172.9 1.0 fusion.26
  174.3 1.0 fusion.25
  175.3 5.1 %reshape.120 = f32[64,16384]{1,0:T(8,128)} reshape(f32[1024,1024]{1,0:T(8,128)} %get-tuple-element.142) | data formatting | bytes 8388608 | tf_op jit(solution)/shard_map/reshape | solution.py:27
  180.4 3.7 fusion.20
  184.2 23.0 %multiply_reduce_fusion.1 = (f32[64,1024]{1,0:T(8,128)}, f32[64,16,1024]{2,1,0:T(8,128)S(1)}, f32[64,16,1024]{2,1,0:T(8,128)}, f32[64,16,1024]{2,1,0:T(8,128)}) fusion(f32[64,16]{1,0:T(8,128)} %get-tuple-element.107, f32[64,1024]{1,0:T(8,128)} %get-tuple-element.75, f32[64,16]{1,0:T(8,128)} %get-tuple-element.123, f32[64,1024]{1,0:T(8,128)S(1)} %get-tuple-element.76, ...), kind=kLoop, calls=%fused_computation.13 | loop fusion | flops 69140480 | bytes 21368832 | tf_op jit(solution)/shard_map/reduce_sum | solution.py:43
  207.9 7.9 %multiply_reduce_fusion.3 = (f32[64,1024]{1,0:T(8,128)}, f32[64,1024]{1,0:T(8,128)}, f32[64,1024]{1,0:T(8,128)}, f32[64,16,1024]{2,1,0:T(8,128)S(1)}) fusion(f32[64,16]{1,0:T(8,128)S(1)} %get-tuple-element.108, f32[64,1024]{1,0:T(8,128)S(1)} %get-tuple-element.76, f32[64,16]{1,0:T(8,128)} %get-tuple-element.124, f32[64,1024]{1,0:T(8,128)S(1)} %get-tuple-element.77, ...), kind=kLoop, calls=%fused_computation.15 | loop fusion | flops 15532032 | bytes 10571776 | tf_op jit(solution)/shard_map/reduce_sum | solution.py:43
  215.8 1.0 slice_multiply_fusion
  216.8 1.0 copy-done.4
  222.1 0.9 pad.41
  223.0 2.2 pad.42
  225.2 1.0 fusion.14
  226.2 1.7 add.323
  227.9 0.9 pad_maximum_fusion.3
  228.8 1.8 pad.44
  230.6 1.3 fusion.13
  231.9 0.9 add.325
  232.8 3.5 pad.45
  236.3 5.7 %pad.46 = f32[16,16,1024]{2,1,0:T(8,128)} pad(f32[8,16,1024]{2,1,0:T(8,128)} %add.325, f32[]{:T(128)} %constant.4.clone.1), padding=1_0_1x0_0_0x0_0_0 | pad | bytes 1572868 | tf_op jit(solution)/shard_map/pad | solution.py:47
  242.0 2.3 fusion.10
  244.4 1.2 add.327
  245.6 1.0 pad_maximum_fusion.1
  246.6 7.0 %pad.47 = f32[32,16,1024]{2,1,0:T(8,128)S(1)} pad(f32[16,16,1024]{2,1,0:T(8,128)} %pad_maximum_fusion.1, f32[]{:T(128)} %constant.4.clone.1), padding=0_1_1x0_0_0x0_0_0 | pad | bytes 3145732 | tf_op jit(solution)/shard_map/pad | solution.py:47
  253.6 10.2 %pad.48 = f32[32,16,1024]{2,1,0:T(8,128)} pad(f32[16,16,1024]{2,1,0:T(8,128)} %add.327, f32[]{:T(128)} %constant.4.clone.1), padding=1_0_1x0_0_0x0_0_0 | pad | bytes 3145732 | tf_op jit(solution)/shard_map/pad | solution.py:47
  263.8 3.9 fusion.9
  267.9 1.7 add.329
  270.6 9.1 %multiply_reduce_fusion.17 = f32[64,1024]{1,0:T(8,128)} fusion(f32[64,16]{1,0:T(8,128)S(1)} %copy-done.96, f32[64,1024]{1,0:T(8,128)S(1)} %copy-done.68, f32[64,16]{1,0:T(8,128)S(1)} %copy-done.120, f32[64,1024]{1,0:T(8,128)S(1)} %copy-done.79, f32[16,1024]{1,0:T(8,128)S(1)} %exponential_negate_fusion, f32[64,1024]{1,0:T(8,128)S(1)} %copy-done.67, ...), kind=kLoop, calls=%fused_computation.29 | loop fusion | flops 35586048 | bytes 4558848 | tf_op jit(solution)/shard_map/reduce_sum | solution.py:43
  279.8 8.2 %multiply_reduce_fusion.19 = f32[64,1024]{1,0:T(8,128)} fusion(f32[64,16]{1,0:T(8,128)S(1)} %copy-done.98, f32[64,1024]{1,0:T(8,128)S(1)} %copy-done.67, f32[64,16]{1,0:T(8,128)S(1)} %copy-done.119, f32[64,1024]{1,0:T(8,128)S(1)} %copy-done.65, f32[64,16]{1,0:T(8,128)S(1)} %copy-done.118, f32[64,1024]{1,0:T(8,128)S(1)} %copy-done.77, ...), kind=kLoop, calls=%fused_computation.31 | loop fusion | flops 31391744 | bytes 4030464 | tf_op jit(solution)/shard_map/reduce_sum | solution.py:43
  287.9 7.0 %multiply_reduce_fusion.21 = f32[64,1024]{1,0:T(8,128)} fusion(f32[64,16]{1,0:T(8,128)S(1)} %copy-done.101, f32[64,1024]{1,0:T(8,128)S(1)} %copy-done.65, f32[64,16]{1,0:T(8,128)S(1)} %copy-done.118, f32[64,1024]{1,0:T(8,128)S(1)} %copy-done.77, f32[16,1024]{1,0:T(8,128)S(1)} %exponential_negate_fusion, f32[64,1024]{1,0:T(8,128)S(1)} %copy-done.57, ...), kind=kLoop, calls=%fused_computation.33 | loop fusion | flops 27197440 | bytes 3502080 | tf_op jit(solution)/shard_map/reduce_sum | solution.py:43
  294.9 1.5 pad_maximum_fusion
  296.4 18.5 %pad.62 = f32[63,16,1024]{2,1,0:T(8,128)} pad(f32[32,16,1024]{2,1,0:T(8,128)} %pad_maximum_fusion, f32[]{:T(128)} %constant.4.clone.1), padding=0_0_1x0_0_0x0_0_0 | pad | bytes 6225924 | tf_op jit(solution)/shard_map/slice | solution.py:48
  314.9 12.1 %pad.86 = f32[64,16,1024]{2,1,0:T(8,128)} pad(f32[32,16,1024]{2,1,0:T(8,128)S(1)} %copy-done.10, f32[]{:T(128)} %constant.4.clone.1), padding=1_0_1x0_0_0x0_0_0 | pad | bytes 6291460
  327.0 4.4 slice_add_fusion.35
  331.7 9.3 %multiply_reduce_fusion.29 = (f32[64,1024]{1,0:T(8,128)S(1)}, f32[64,1024]{1,0:T(8,128)S(1)}, f32[64,1024]{1,0:T(8,128)S(1)}, f32[64,1024]{1,0:T(8,128)S(1)}, f32[64,1024]{1,0:T(8,128)S(1)}, /*index=5*/f32[64,1024]{1,0:T(8,128)S(1)}) fusion(f32[64,16]{1,0:T(8,128)S(1)} %copy-done.106, f32[64,1024]{1,0:T(8,128)S(1)} %copy-done.62, ...), kind=kLoop, calls=%fused_computation.41 | loop fusion | flops 27918336 | bytes 7630848 | tf_op jit(solution)/shard_map/reduce_sum | solution.py:43
  341.9 7.3 %multiply_reduce_fusion.23 = (f32[64,1024]{1,0:T(8,128)S(1)}, f32[64,1024]{1,0:T(8,128)S(1)}, f32[64,1024]{1,0:T(8,128)S(1)}) fusion(f32[64,16]{1,0:T(8,128)S(1)} %copy-done.103, f32[64,1024]{1,0:T(8,128)S(1)} %copy-done.58, f32[64,16]{1,0:T(8,128)S(1)} %copy-done.110, f32[64,1024]{1,0:T(8,128)S(1)} %copy-done.60, f32[64,16]{1,0:T(8,128)S(1)} %copy-done.112, ...), kind=kLoop, calls=%fused_computation.35 | loop fusion | flops 27066368 | bytes 3506176 | tf_op jit(solution)/shard_map/reduce_sum | solution.py:43
  349.4 9.2 %multiply_reduce_fusion = (f32[64,1024]{1,0:T(8,128)S(1)}, f32[64,1024]{1,0:T(8,128)S(1)}, f32[64,1024]{1,0:T(8,128)S(1)}, f32[64,1024]{1,0:T(8,128)S(1)}, f32[64,1024]{1,0:T(8,128)S(1)}, /*index=5*/f32[64,1024]{1,0:T(8,128)S(1)}) fusion(f32[64,16]{1,0:T(8,128)S(1)} %copy-done.100, f32[16,1024]{1,0:T(8,128)S(1)} %exponential_negate_fusion, ...), kind=kLoop, calls=%fused_computation.12 | loop fusion | flops 24772608 | bytes 7364608 | tf_op jit(solution)/shard_map/reduce_sum | solution.py:52
  358.6 0.7 add_dynamic-update-slice_fusion.14
  360.1 0.7 add_dynamic-update-slice_fusion.12
  360.9 0.7 add_dynamic-update-slice_fusion.11
  362.4 5.9 %multiply_reduce_fusion.9 = (f32[64,1024]{1,0:T(8,128)S(1)}, f32[64,1024]{1,0:T(8,128)S(1)}, f32[64,1024]{1,0:T(8,128)S(1)}, f32[64,1024]{1,0:T(8,128)S(1)}) fusion(f32[64,16]{1,0:T(8,128)S(1)} %copy-done.90, f32[64,1024]{1,0:T(8,128)S(1)} %copy-done.16, f32[64,16]{1,0:T(8,128)S(1)} %copy-done.86, f32[64,1024]{1,0:T(8,128)S(1)} %copy-done.26, ...), kind=kLoop, calls=%fused_computation.21 | loop fusion | flops 20709376 | bytes 6909952 | tf_op jit(solution)/shard_map/reduce_sum | solution.py:43
  368.4 9.0 %multiply_reduce_fusion.2 = (f32[64,1024]{1,0:T(8,128)S(1)}, f32[64,1024]{1,0:T(8,128)S(1)}, f32[64,1024]{1,0:T(8,128)S(1)}, f32[64,1024]{1,0:T(8,128)S(1)}, f32[64,1024]{1,0:T(8,128)S(1)}, /*index=5*/f32[64,1024]{1,0:T(8,128)S(1)}) fusion(f32[64,1024]{1,0:T(8,128)S(1)} %copy-done.33, f32[64,16]{1,0:T(8,128)S(1)} %copy-done.82, ...), kind=kLoop, calls=%fused_computation.14 | loop fusion | flops 24772608 | bytes 7364608 | tf_op jit(solution)/shard_map/reduce_sum | solution.py:52
  377.5 0.7 add_dynamic-update-slice_fusion.9
  378.2 0.7 add_dynamic-update-slice_fusion.8
  381.2 0.7 add_dynamic-update-slice_fusion.4
  382.6 0.8 add_dynamic-update-slice_fusion.2
  383.4 0.7 add_dynamic-update-slice_fusion.1
  384.1 0.7 add_dynamic-update-slice_fusion
  384.9 5.0 %reshape.121 = f32[1024,1024]{1,0:T(8,128)} reshape(f32[64,16384]{1,0:T(8,128)} %add_dynamic-update-slice_fusion) | data formatting | bytes 8388608 | tf_op jit(solution)/shard_map/reshape | solution.py:56
  389.9 9.1 %fusion.1 = bf16[1024,1024]{1,0:T(8,128)(2,1)S(1)} fusion(f32[1024,1024]{1,0:T(8,128)} %reshape.121, f32[1024]{0:T(1024)S(1)} %copy-done.122, f32[1024,1024]{1,0:T(8,128)} %bitcast.20, f32[1024]{0:T(1024)S(1)} %bitcast.30, f32[1024]{0:T(1024)S(1)} %bitcast.32, f32[1024]{0:T(1024)S(1)} %bitcast.28, f32[1024]{0:T(1024)S(1)} %bitcast.26, ...), kind=kLoop, calls=%fused_computation.6 | loop fusion | flops 17825792 | bytes 10510336 | tf_op jit(solution)/shard_map/convert_element_type | solution.py:93
  399.0 51.4 %all_to_all.26 = bf16[8,128,1024]{2,1,0:T(8,128)(2,1)S(1)} all-to-all(bf16[8,128,1024]{2,1,0:T(8,128)(2,1)S(1)} %bitcast.23), channel_id=1, replica_groups=mesh['seq'=8,'batch'=4] {'seq'}, dimensions={0} | all-to-all | bytes 4194304 | tf_op jit(solution)/shard_map/all_to_all | solution.py:94
  451.2 1.3 copy-done.14
  452.5 2.5 fusion.8
  (285 shorter events, 14.0 us)
Async XLA Ops:
  6.5 63.9 %copy-start = (bf16[1024,288]{0,1:T(8,128)(2,1)S(1)}, bf16[1024,288]{0,1:T(8,128)(2,1)}, u32[]{:S(2)}) copy-start(bf16[1024,288]{0,1:T(8,128)(2,1)} %param.14) | copy-start | bytes 1769476
  6.5 10.6 %copy-start.123 = (bf16[1024]{0:T(1024)(128)(2,1)S(1)}, bf16[1024]{0:T(1024)(128)(2,1)}, u32[]{:S(2)}) copy-start(bf16[1024]{0:T(1024)(128)(2,1)} %param.13) | copy-start | bytes 6148
  6.5 10.6 %copy-start.121 = (bf16[4,1024]{1,0:T(4,128)(2,1)S(1)}, bf16[4,1024]{1,0:T(4,128)(2,1)}, u32[]{:S(2)}) copy-start(bf16[4,1024]{1,0:T(4,128)(2,1)} %param.12) | copy-start | bytes 24580
  9.8 55.5 %all-to-all-start = ((bf16[128,8,1024]{2,0,1:T(8,128)(2,1)}), bf16[128,8,1024]{2,0,1:T(8,128)(2,1)S(1)}, u32[]{:S(2)}, u32[]{:S(2)}) async-start(bf16[128,8,1024]{2,0,1:T(8,128)(2,1)} %bitcast.22), calls=%async_computation | async-start | bytes 4194304 | tf_op jit(solution)/shard_map/all_to_all | solution.py:74
  17.1 134.9 %all-reduce.16.cloned.1.call-start = ((), (), s32[]{:S(2)}) async-start(), calls=%async_computation.2 | async-start | bytes 2359296 | tf_op jit(solution)/shard_map/psum | solution.py:78
  17.2 48.6 %copy-start.94 = (f32[1,1024]{1,0:T(1,128)}, f32[1,1024]{1,0:T(1,128)S(1)}, u32[]{:S(2)}) copy-start(f32[1,1024]{1,0:T(1,128)S(1)} %get-tuple-element.141) | copy-start | bytes 12292
  70.5 82.8 %copy-start.124 = (bf16[256,1024]{1,0:T(8,128)(2,1)S(1)}, bf16[256,1024]{1,0:T(8,128)(2,1)}, u32[]{:S(2)}) copy-start(bf16[256,1024]{1,0:T(8,128)(2,1)} %param.16) | copy-start | bytes 1572868
  70.5 82.8 %copy-start.125 = (f32[1024]{0:T(1024)S(1)}, f32[1024]{0:T(1024)}, u32[]{:S(2)}) copy-start(f32[1024]{0:T(1024)} %param.17) | copy-start | bytes 12292
  70.5 82.8 %copy-start.126 = (f32[256]{0:T(256)S(1)}, f32[256]{0:T(256)}, u32[]{:S(2)}) copy-start(f32[256]{0:T(256)} %param.15) | copy-start | bytes 3076
  169.3 14.9 %copy-start.21 = (f32[64,1024]{1,0:T(8,128)}, f32[64,1024]{1,0:T(8,128)S(1)}, u32[]{:S(2)}) copy-start(f32[64,1024]{1,0:T(8,128)S(1)} %get-tuple-element.66) | copy-start | bytes 786436
  169.3 14.9 %copy-start.23 = (f32[64,1024]{1,0:T(8,128)}, f32[64,1024]{1,0:T(8,128)S(1)}, u32[]{:S(2)}) copy-start(f32[64,1024]{1,0:T(8,128)S(1)} %get-tuple-element.67) | copy-start | bytes 786436
  169.3 14.9 %copy-start.25 = (f32[64,1024]{1,0:T(8,128)}, f32[64,1024]{1,0:T(8,128)S(1)}, u32[]{:S(2)}) copy-start(f32[64,1024]{1,0:T(8,128)S(1)} %get-tuple-element.68) | copy-start | bytes 786436
  171.4 12.8 %copy-start.45 = (f32[64,1024]{1,0:T(8,128)}, f32[64,1024]{1,0:T(8,128)S(1)}, u32[]{:S(2)}) copy-start(f32[64,1024]{1,0:T(8,128)S(1)} %get-tuple-element.58) | copy-start | bytes 786436
  171.4 12.8 %copy-start.47 = (f32[64,1024]{1,0:T(8,128)}, f32[64,1024]{1,0:T(8,128)S(1)}, u32[]{:S(2)}) copy-start(f32[64,1024]{1,0:T(8,128)S(1)} %get-tuple-element.59) | copy-start | bytes 786436
  171.4 12.8 %copy-start.49 = (f32[64,1024]{1,0:T(8,128)}, f32[64,1024]{1,0:T(8,128)S(1)}, u32[]{:S(2)}) copy-start(f32[64,1024]{1,0:T(8,128)S(1)} %get-tuple-element.60) | copy-start | bytes 786436
  171.4 36.5 %copy-start.28 = (f32[64,1024]{1,0:T(8,128)}, f32[64,1024]{1,0:T(8,128)S(1)}, u32[]{:S(2)}) copy-start(f32[64,1024]{1,0:T(8,128)S(1)} %get-tuple-element.41) | copy-start | bytes 786436
  175.3 32.6 %copy-start.81 = (f32[64,16]{1,0:T(8,128)}, f32[64,16]{1,0:T(8,128)S(1)}, u32[]{:S(2)}) copy-start(f32[64,16]{1,0:T(8,128)S(1)} %get-tuple-element.108) | copy-start | bytes 12292
  184.1 23.1 %copy-start.15 = (f32[64,1024]{1,0:T(8,128)}, f32[64,1024]{1,0:T(8,128)S(1)}, u32[]{:S(2)}) copy-start(f32[64,1024]{1,0:T(8,128)S(1)} %get-tuple-element.79) | copy-start | bytes 786436
  184.1 23.1 %copy-start.17 = (f32[64,1024]{1,0:T(8,128)}, f32[64,1024]{1,0:T(8,128)S(1)}, u32[]{:S(2)}) copy-start(f32[64,1024]{1,0:T(8,128)S(1)} %get-tuple-element.80) | copy-start | bytes 786436
  184.1 23.1 %copy-start.19 = (f32[64,1024]{1,0:T(8,128)}, f32[64,1024]{1,0:T(8,128)S(1)}, u32[]{:S(2)}) copy-start(f32[64,1024]{1,0:T(8,128)S(1)} %get-tuple-element.81) | copy-start | bytes 786436
  184.1 23.1 %copy-start.54 = (f32[64,1024]{1,0:T(8,128)}, f32[64,1024]{1,0:T(8,128)S(1)}, u32[]{:S(2)}) copy-start(f32[64,1024]{1,0:T(8,128)S(1)} %get-tuple-element.74) | copy-start | bytes 786436
  207.2 8.6 %copy-start.7 = (f32[64,16,1024]{2,1,0:T(8,128)}, f32[64,16,1024]{2,1,0:T(8,128)S(1)}, u32[]{:S(2)}) copy-start(f32[64,16,1024]{2,1,0:T(8,128)S(1)} %get-tuple-element.38) | copy-start | bytes 12582916
  222.1 10.7 %copy-start.72 = (f32[1,16,1024]{2,1,0:T(8,128)S(1)}, f32[1,16,1024]{2,1,0:T(8,128)}, u32[]{:S(2)}) copy-start(f32[1,16,1024]{2,1,0:T(8,128)} %slice.548) | copy-start | bytes 196612
  270.6 9.1 %copy-start.98 = (f32[64,16]{1,0:T(8,128)S(1)}, f32[64,16]{1,0:T(8,128)}, u32[]{:S(2)}) copy-start(f32[64,16]{1,0:T(8,128)} %get-tuple-element.115) | copy-start | bytes 12292
  279.7 8.2 %copy-start.101 = (f32[64,16]{1,0:T(8,128)S(1)}, f32[64,16]{1,0:T(8,128)}, u32[]{:S(2)}) copy-start(f32[64,16]{1,0:T(8,128)} %get-tuple-element.116) | copy-start | bytes 12292
  294.9 19.9 %copy-start.10 = (f32[32,16,1024]{2,1,0:T(8,128)S(1)}, f32[32,16,1024]{2,1,0:T(8,128)}, u32[]{:S(2)}) copy-start(f32[32,16,1024]{2,1,0:T(8,128)} %add.329) | copy-start | bytes 6291460
  331.6 10.1 %copy-start.56 = (f32[64,1024]{1,0:T(8,128)S(1)}, f32[64,1024]{1,0:T(8,128)}, u32[]{:S(2)}) copy-start(f32[64,1024]{1,0:T(8,128)} %copy-done.54) | copy-start | bytes 786436
  331.6 10.1 %copy-start.58 = (f32[64,1024]{1,0:T(8,128)S(1)}, f32[64,1024]{1,0:T(8,128)}, u32[]{:S(2)}) copy-start(f32[64,1024]{1,0:T(8,128)} %get-tuple-element.86) | copy-start | bytes 786436
  331.6 10.1 %copy-start.60 = (f32[64,1024]{1,0:T(8,128)S(1)}, f32[64,1024]{1,0:T(8,128)}, u32[]{:S(2)}) copy-start(f32[64,1024]{1,0:T(8,128)} %get-tuple-element.87) | copy-start | bytes 786436
  331.6 10.1 %copy-start.74 = (f32[64,1024]{1,0:T(8,128)S(1)}, f32[64,1024]{1,0:T(8,128)}, u32[]{:S(2)}) copy-start(f32[64,1024]{1,0:T(8,128)} %get-tuple-element.62) | copy-start | bytes 786436
  331.6 10.1 %copy-start.103 = (f32[64,16]{1,0:T(8,128)S(1)}, f32[64,16]{1,0:T(8,128)}, u32[]{:S(2)}) copy-start(f32[64,16]{1,0:T(8,128)} %get-tuple-element.117) | copy-start | bytes 12292
  331.7 10.1 %copy-start.104 = (f32[64,16]{1,0:T(8,128)S(1)}, f32[64,16]{1,0:T(8,128)}, u32[]{:S(2)}) copy-start(f32[64,16]{1,0:T(8,128)} %get-tuple-element.118) | copy-start | bytes 12292
  331.7 10.1 %copy-start.105 = (f32[64,16]{1,0:T(8,128)S(1)}, f32[64,16]{1,0:T(8,128)}, u32[]{:S(2)}) copy-start(f32[64,16]{1,0:T(8,128)} %get-tuple-element.119) | copy-start | bytes 12292
  331.7 10.1 %copy-start.108 = (f32[64,16]{1,0:T(8,128)S(1)}, f32[64,16]{1,0:T(8,128)}, u32[]{:S(2)}) copy-start(f32[64,16]{1,0:T(8,128)} %get-tuple-element.122) | copy-start | bytes 12292
  331.7 10.1 %copy-start.110 = (f32[64,16]{1,0:T(8,128)S(1)}, f32[64,16]{1,0:T(8,128)}, u32[]{:S(2)}) copy-start(f32[64,16]{1,0:T(8,128)} %get-tuple-element.134) | copy-start | bytes 12292
  331.7 10.1 %copy-start.112 = (f32[64,16]{1,0:T(8,128)S(1)}, f32[64,16]{1,0:T(8,128)}, u32[]{:S(2)}) copy-start(f32[64,16]{1,0:T(8,128)} %get-tuple-element.135) | copy-start | bytes 12292
  341.8 7.4 %copy-start.29 = (f32[64,1024]{1,0:T(8,128)S(1)}, f32[64,1024]{1,0:T(8,128)}, u32[]{:S(2)}) copy-start(f32[64,1024]{1,0:T(8,128)} %copy-done.28) | copy-start | bytes 786436
  341.8 7.4 %copy-start.40 = (f32[64,1024]{1,0:T(8,128)S(1)}, f32[64,1024]{1,0:T(8,128)}, u32[]{:S(2)}) copy-start(f32[64,1024]{1,0:T(8,128)} %get-tuple-element.51) | copy-start | bytes 786436
  341.8 7.4 %copy-start.41 = (f32[64,1024]{1,0:T(8,128)S(1)}, f32[64,1024]{1,0:T(8,128)}, u32[]{:S(2)}) copy-start(f32[64,1024]{1,0:T(8,128)} %get-tuple-element.52) | copy-start | bytes 786436
  349.3 12.4 %copy-start.70 = (f32[64,1024]{1,0:T(8,128)S(1)}, f32[64,1024]{1,0:T(8,128)}, u32[]{:S(2)}) copy-start(f32[64,1024]{1,0:T(8,128)} %multiply_reduce_fusion.21) | copy-start | bytes 786436
  349.3 13.1 %copy-start.13 = (f32[64,16,1024]{2,1,0:T(8,128)S(1)}, f32[64,16,1024]{2,1,0:T(8,128)}, u32[]{:S(2)}) copy-start(f32[64,16,1024]{2,1,0:T(8,128)} %get-tuple-element.40) | copy-start | bytes 12582916
  349.3 13.1 %copy-start.16 = (f32[64,1024]{1,0:T(8,128)S(1)}, f32[64,1024]{1,0:T(8,128)}, u32[]{:S(2)}) copy-start(f32[64,1024]{1,0:T(8,128)} %copy-done.15) | copy-start | bytes 786436
  349.3 13.1 %copy-start.18 = (f32[64,1024]{1,0:T(8,128)S(1)}, f32[64,1024]{1,0:T(8,128)}, u32[]{:S(2)}) copy-start(f32[64,1024]{1,0:T(8,128)} %copy-done.17) | copy-start | bytes 786436
  349.3 13.1 %copy-start.20 = (f32[64,1024]{1,0:T(8,128)S(1)}, f32[64,1024]{1,0:T(8,128)}, u32[]{:S(2)}) copy-start(f32[64,1024]{1,0:T(8,128)} %copy-done.19) | copy-start | bytes 786436
  349.3 13.1 %copy-start.22 = (f32[64,1024]{1,0:T(8,128)S(1)}, f32[64,1024]{1,0:T(8,128)}, u32[]{:S(2)}) copy-start(f32[64,1024]{1,0:T(8,128)} %copy-done.21) | copy-start | bytes 786436
  349.3 13.1 %copy-start.24 = (f32[64,1024]{1,0:T(8,128)S(1)}, f32[64,1024]{1,0:T(8,128)}, u32[]{:S(2)}) copy-start(f32[64,1024]{1,0:T(8,128)} %copy-done.23) | copy-start | bytes 786436
  349.3 13.1 %copy-start.26 = (f32[64,1024]{1,0:T(8,128)S(1)}, f32[64,1024]{1,0:T(8,128)}, u32[]{:S(2)}) copy-start(f32[64,1024]{1,0:T(8,128)} %copy-done.25) | copy-start | bytes 786436
  349.3 13.1 %copy-start.80 = (f32[64,16]{1,0:T(8,128)S(1)}, f32[64,16]{1,0:T(8,128)}, u32[]{:S(2)}) copy-start(f32[64,16]{1,0:T(8,128)} %get-tuple-element.106) | copy-start | bytes 12292
  349.3 13.1 %copy-start.83 = (f32[64,16]{1,0:T(8,128)S(1)}, f32[64,16]{1,0:T(8,128)}, u32[]{:S(2)}) copy-start(f32[64,16]{1,0:T(8,128)} %get-tuple-element.112) | copy-start | bytes 12292
  349.4 13.1 %copy-start.84 = (f32[64,16]{1,0:T(8,128)S(1)}, f32[64,16]{1,0:T(8,128)}, u32[]{:S(2)}) copy-start(f32[64,16]{1,0:T(8,128)} %get-tuple-element.113) | copy-start | bytes 12292
  349.4 13.1 %copy-start.86 = (f32[64,16]{1,0:T(8,128)S(1)}, f32[64,16]{1,0:T(8,128)}, u32[]{:S(2)}) copy-start(f32[64,16]{1,0:T(8,128)} %get-tuple-element.127) | copy-start | bytes 12292
  349.4 13.1 %copy-start.88 = (f32[64,16]{1,0:T(8,128)S(1)}, f32[64,16]{1,0:T(8,128)}, u32[]{:S(2)}) copy-start(f32[64,16]{1,0:T(8,128)} %get-tuple-element.128) | copy-start | bytes 12292
  349.4 13.1 %copy-start.89 = (f32[64,16]{1,0:T(8,128)S(1)}, f32[64,16]{1,0:T(8,128)}, u32[]{:S(2)}) copy-start(f32[64,16]{1,0:T(8,128)} %get-tuple-element.129) | copy-start | bytes 12292
  360.8 7.5 %copy-start.33 = (f32[64,1024]{1,0:T(8,128)S(1)}, f32[64,1024]{1,0:T(8,128)}, u32[]{:S(2)}) copy-start(f32[64,1024]{1,0:T(8,128)} %get-tuple-element.42) | copy-start | bytes 786436
  360.8 7.5 %copy-start.34 = (f32[64,1024]{1,0:T(8,128)S(1)}, f32[64,1024]{1,0:T(8,128)}, u32[]{:S(2)}) copy-start(f32[64,1024]{1,0:T(8,128)} %get-tuple-element.46) | copy-start | bytes 786436
  360.8 7.5 %copy-start.35 = (f32[64,1024]{1,0:T(8,128)S(1)}, f32[64,1024]{1,0:T(8,128)}, u32[]{:S(2)}) copy-start(f32[64,1024]{1,0:T(8,128)} %get-tuple-element.47) | copy-start | bytes 786436
  360.8 7.5 %copy-start.36 = (f32[64,1024]{1,0:T(8,128)S(1)}, f32[64,1024]{1,0:T(8,128)}, u32[]{:S(2)}) copy-start(f32[64,1024]{1,0:T(8,128)} %get-tuple-element.48) | copy-start | bytes 786436
  360.8 7.5 %copy-start.37 = (f32[64,1024]{1,0:T(8,128)S(1)}, f32[64,1024]{1,0:T(8,128)}, u32[]{:S(2)}) copy-start(f32[64,1024]{1,0:T(8,128)} %get-tuple-element.49) | copy-start | bytes 786436
  360.8 7.5 %copy-start.38 = (f32[64,1024]{1,0:T(8,128)S(1)}, f32[64,1024]{1,0:T(8,128)}, u32[]{:S(2)}) copy-start(f32[64,1024]{1,0:T(8,128)} %get-tuple-element.50) | copy-start | bytes 786436
  360.9 7.5 %copy-start.82 = (f32[64,16]{1,0:T(8,128)S(1)}, f32[64,16]{1,0:T(8,128)}, u32[]{:S(2)}) copy-start(f32[64,16]{1,0:T(8,128)} %copy-done.81) | copy-start | bytes 12292
  360.9 7.5 %copy-start.97 = (f32[64,16]{1,0:T(8,128)S(1)}, f32[64,16]{1,0:T(8,128)}, u32[]{:S(2)}) copy-start(f32[64,16]{1,0:T(8,128)} %get-tuple-element.114) | copy-start | bytes 12292
  360.9 7.5 %copy-start.99 = (f32[64,16]{1,0:T(8,128)S(1)}, f32[64,16]{1,0:T(8,128)}, u32[]{:S(2)}) copy-start(f32[64,16]{1,0:T(8,128)} %get-tuple-element.115) | copy-start | bytes 12292
  368.4 9.1 %copy-start.69 = (f32[64,1024]{1,0:T(8,128)S(1)}, f32[64,1024]{1,0:T(8,128)}, u32[]{:S(2)}) copy-start(f32[64,1024]{1,0:T(8,128)} %multiply_reduce_fusion.19) | copy-start | bytes 786436
  368.4 9.8 %copy-start.66 = (f32[64,1024]{1,0:T(8,128)S(1)}, f32[64,1024]{1,0:T(8,128)}, u32[]{:S(2)}) copy-start(f32[64,1024]{1,0:T(8,128)} %multiply_reduce_fusion.17) | copy-start | bytes 786436
  (65 other events, 234.3 us)
Sparse Core Ops, SparseCore 0:
  72.5 79.4 all-reduce.15
where the time goes:
time: 465 us; the launch traced here: 462 us
  other arithmetic  151 us (32%)
  waiting for transfers between devices  128 us (28%)
  local copies, waits for them, and re-layouts  100 us (22%)
  blocking collectives  51.4 us (11%)
  between operations  15 us (3%)
  matrix products  9.11 us (2%)
  starting transfers between devices  7.35 us (2%)
    psum x1, waiting for transfers between devices, local(): proj = lax.psum(partial_value, 'seq')  79.5 us
    reduce_sum x8, other arithmetic, selective_scan(): local_parts.append(jnp.sum(c_now[:, :, None] * state, axis=1))  77.7 us
    all_to_all x1, blocking collectives, local(): lax.all_to_all(y_out, 'seq', split_axis=0, concat_axis=1, tiled=True)  51.4 us
    all_to_all x1, waiting for transfers between devices, local(): lax.all_to_all(conv_input, 'seq', split_axis=1, concat_axis=0, tiled=True)  48.1 us
    pad x8, local copies, waits for them, and re-layouts, selective_scan(): _, through = lax.associative_scan(link_blocks, (totals, state), axis=0)  31.3 us
    slice x1, local copies, waits for them, and re-layouts, selective_scan(): through[:blocks - 1]  18.5 us
    unnamed x255, local copies, waits for them, and re-layouts  18.3 us
    reduce_sum x2, other arithmetic, selective_scan(): jnp.sum(c_now[:, :, None] * jnp.exp(elapsed[place][:, None, :] * rate[Non...  18.2 us
  transfers between devices with their start and end apart: 2, of which 2 were waited for; matrix products, arithmetic and copies ran while one was open for 0% of the time, Pallas kernels for 0%

commit v1 on v0

--- a/solution.py
+++ b/solution.py
@@ -2,6 +2,10 @@
 import jax.numpy as jnp
 from jax import lax
 from jax.sharding import PartitionSpec as P
+
+
+def advance_the_axis_part(piece_in):
+    return jnp.sum(jax.lax.all_gather(piece_in, "seq"), axis=0)
 
 
 def causal_conv(prefix, inputs, weight, bias):
@@ -75,7 +79,7 @@
     zero_prefix = jnp.zeros((width - 1, arrived.shape[1]), jnp.float32)
     conv_out = causal_conv(zero_prefix, arrived, conv_weight, conv_bias)
     partial_value = jnp.dot(conv_out, x_weight, preferred_element_type=jnp.float32)
-    proj = lax.psum(partial_value, "seq")
+    proj = advance_the_axis_part(partial_value)
     dt_low = proj[:, :rank]
     bmat = proj[:, rank : rank + states]
     cmat = proj[:, rank + states :]

time: 465 us -> 536 us (1.15)
  waiting for transfers between devices: 128 us -> 185 us
  local copies, waits for them, and re-layouts: 100 us -> 112 us
    all_gather x0 -> x1, waiting for transfers between devices: none -> 136 us  [advance_the_axis_part(): return jnp.sum(jax.lax.all_gather(piece_in, 'seq'), axis=0)]
    psum x1 -> x0, waiting for transfers between devices: 79.5 us -> none  [local(): proj = lax.psum(partial_value, 'seq')]
    unnamed x255 -> x256, local copies, waits for them, and re-layouts: 18.3 us -> 30.6 us
where the time goes in v1:
time: 536 us; the launch traced here: 530 us
  waiting for transfers between devices  185 us (35%)
  other arithmetic  153 us (29%)
  local copies, waits for them, and re-layouts  112 us (21%)
  blocking collectives  50.8 us (9%)
  between operations  15.3 us (3%)
  matrix products  7.91 us (1%)
  starting transfers between devices  7.35 us (1%)
    all_gather x1, waiting for transfers between devices, advance_the_axis_part(): return jnp.sum(jax.lax.all_gather(piece_in, 'seq'), axis=0)  136 us
    reduce_sum x8, other arithmetic, selective_scan(): local_parts.append(jnp.sum(c_now[:, :, None] * state, axis=1))  77.7 us
    all_to_all x1, blocking collectives, local(): lax.all_to_all(y_out, 'seq', split_axis=0, concat_axis=1, tiled=True)  50.8 us
    all_to_all x1, waiting for transfers between devices, local(): lax.all_to_all(conv_input, 'seq', split_axis=1, concat_axis=0, tiled=True)  48.1 us
    pad x8, local copies, waits for them, and re-layouts, selective_scan(): _, through = lax.associative_scan(link_blocks, (totals, state), axis=0)  31.5 us
    unnamed x256, local copies, waits for them, and re-layouts  30.6 us
    slice x1, local copies, waits for them, and re-layouts, selective_scan(): through[:blocks - 1]  18.5 us
    reduce_sum x2, other arithmetic, selective_scan(): jnp.sum(c_now[:, :, None] * jnp.exp(elapsed[place][:, None, :] * rate[Non...  18 us
  transfers between devices with their start and end apart: 2, of which 2 were waited for; matrix products, arithmetic and copies ran while one was open for 0% of the time, Pallas kernels for 0%

profile of v1, /device:TPU:0, one launch (start us, length us, event | category | flops | bytes accessed | tf_op | source)
XLA Modules:
  0.0 530.3 jit_solution(9766599887796713287)
XLA Ops:
  6.5 3.2 copy.27
  9.8 7.3 %all-to-all-start = ((bf16[128,8,1024]{2,0,1:T(8,128)(2,1)}), bf16[128,8,1024]{2,0,1:T(8,128)(2,1)S(1)}, u32[]{:S(2)}, u32[]{:S(2)}) async-start(bf16[128,8,1024]{2,0,1:T(8,128)(2,1)} %bitcast.28), calls=%async_computation | async-start | bytes 4194304 | tf_op jit(solution)/shard_map/all_to_all | solution.py:78
  17.2 48.1 %all-to-all-done = bf16[128,8,1024]{2,0,1:T(8,128)(2,1)S(1)} async-done(((bf16[128,8,1024]{2,0,1:T(8,128)(2,1)}), bf16[128,8,1024]{2,0,1:T(8,128)(2,1)S(1)}, u32[]{:S(2)}, u32[]{:S(2)}) %all-to-all-start) | async-done | bytes 2097184 | tf_op jit(solution)/shard_map/all_to_all | solution.py:78
  65.8 1.9 copy-done.2
  67.7 3.2 multiply_convert_fusion
  71.0 1.8 fusion.27
  72.9 136.4 %all-gather.3.cloned.1.call-done = f32[8192,288]{0,1:T(8,128)} async-done(((f32[1024,288]{0,1:T(8,128)}), f32[8192,288]{0,1:T(8,128)}) %all-gather.3.cloned.1.call-update) | async-done | bytes 9437200 | tf_op jit(solution)/shard_map/all_gather | solution.py:8
  209.3 12.3 %copy.25 = f32[36,8,8,1024]{3,2,1,0:T(8,128)S(1)} copy(f32[36,8,8,1024]{3,1,2,0:T(8,128)} %bitcast.27) | data formatting | bytes 18874368
  221.7 2.4 bitcast_reduce_fusion
  224.3 6.1 %convert_multiply_fusion.2 = (f32[1024,1024]{1,0:T(8,128)}, f32[1024,1024]{1,0:T(8,128)}) fusion(bf16[1024,1024]{1,0:T(8,128)(2,1)S(1)} %multiply_convert_fusion, f32[1024]{0:T(1024)S(1)} %copy-done.125, bf16[256,1024]{1,0:T(8,128)(2,1)S(1)} %copy-done.124, f32[1024,288]{0,1:T(8,128)S(1)} %bitcast_reduce_fusion, f32[256]{0:T(256)S(1)} %copy-done.126, ...), kind=kOutput, calls=%fused_computation.5 | convolution fusion | flops 547094528 | bytes 12067840 | tf_op jit(solution)/shard_map/dot_general | solution.py:92
  230.3 5.0 reshape.118
  235.3 3.4 fusion.19
  239.0 2.1 slice_add_fusion.20
  241.6 1.0 fusion.26
  243.0 1.0 fusion.25
  244.0 5.1 reshape.120
  249.1 3.7 fusion.20
  252.9 23.0 %multiply_reduce_fusion.1 = (f32[64,1024]{1,0:T(8,128)}, f32[64,16,1024]{2,1,0:T(8,128)S(1)}, f32[64,16,1024]{2,1,0:T(8,128)}, f32[64,16,1024]{2,1,0:T(8,128)}) fusion(f32[64,16]{1,0:T(8,128)} %get-tuple-element.107, f32[64,1024]{1,0:T(8,128)} %get-tuple-element.75, f32[64,16]{1,0:T(8,128)} %get-tuple-element.123, f32[64,1024]{1,0:T(8,128)S(1)} %get-tuple-element.76, ...), kind=kLoop, calls=%fused_computation.14 | loop fusion | flops 69140480 | bytes 21368832 | tf_op jit(solution)/shard_map/reduce_sum | solution.py:47
  276.6 7.8 %multiply_reduce_fusion.3 = (f32[64,1024]{1,0:T(8,128)}, f32[64,1024]{1,0:T(8,128)}, f32[64,1024]{1,0:T(8,128)}, f32[64,16,1024]{2,1,0:T(8,128)S(1)}) fusion(f32[64,16]{1,0:T(8,128)S(1)} %get-tuple-element.108, f32[64,1024]{1,0:T(8,128)S(1)} %get-tuple-element.76, f32[64,16]{1,0:T(8,128)} %get-tuple-element.124, f32[64,1024]{1,0:T(8,128)S(1)} %get-tuple-element.77, ...), kind=kLoop, calls=%fused_computation.16 | loop fusion | flops 15532032 | bytes 10571776 | tf_op jit(solution)/shard_map/reduce_sum | solution.py:47
  284.4 1.0 slice_multiply_fusion
  285.3 1.0 copy-done.4
  290.6 0.9 pad.41
  291.5 2.2 pad.42
  293.8 1.0 fusion.14
  294.7 1.7 add.321
  296.4 0.9 pad_maximum_fusion.3
  297.3 1.8 pad.44
  299.1 1.3 fusion.13
  300.4 0.9 add.323
  301.3 3.5 pad.45
  304.8 5.9 %pad.46 = f32[16,16,1024]{2,1,0:T(8,128)} pad(f32[8,16,1024]{2,1,0:T(8,128)} %add.323, f32[]{:T(128)} %constant.4.clone.1), padding=1_0_1x0_0_0x0_0_0 | pad | bytes 1572868 | tf_op jit(solution)/shard_map/pad | solution.py:51
  310.7 2.3 fusion.10
  313.1 1.2 add.325
  314.3 1.0 pad_maximum_fusion.1
  315.4 7.0 %pad.47 = f32[32,16,1024]{2,1,0:T(8,128)S(1)} pad(f32[16,16,1024]{2,1,0:T(8,128)} %pad_maximum_fusion.1, f32[]{:T(128)} %constant.4.clone.1), padding=0_1_1x0_0_0x0_0_0 | pad | bytes 3145732 | tf_op jit(solution)/shard_map/pad | solution.py:51
  322.3 10.2 %pad.48 = f32[32,16,1024]{2,1,0:T(8,128)} pad(f32[16,16,1024]{2,1,0:T(8,128)} %add.325, f32[]{:T(128)} %constant.4.clone.1), padding=1_0_1x0_0_0x0_0_0 | pad | bytes 3145732 | tf_op jit(solution)/shard_map/pad | solution.py:51
  332.5 3.9 fusion.9
  336.6 1.7 add.327
  339.4 9.1 %multiply_reduce_fusion.17 = f32[64,1024]{1,0:T(8,128)} fusion(f32[64,16]{1,0:T(8,128)S(1)} %copy-done.96, f32[64,1024]{1,0:T(8,128)S(1)} %copy-done.68, f32[64,16]{1,0:T(8,128)S(1)} %copy-done.120, f32[64,1024]{1,0:T(8,128)S(1)} %copy-done.79, f32[16,1024]{1,0:T(8,128)S(1)} %exponential_negate_fusion, f32[64,1024]{1,0:T(8,128)S(1)} %copy-done.67, ...), kind=kLoop, calls=%fused_computation.30 | loop fusion | flops 35586048 | bytes 4558848 | tf_op jit(solution)/shard_map/reduce_sum | solution.py:47
  348.5 8.2 %multiply_reduce_fusion.19 = f32[64,1024]{1,0:T(8,128)} fusion(f32[64,16]{1,0:T(8,128)S(1)} %copy-done.98, f32[64,1024]{1,0:T(8,128)S(1)} %copy-done.67, f32[64,16]{1,0:T(8,128)S(1)} %copy-done.119, f32[64,1024]{1,0:T(8,128)S(1)} %copy-done.65, f32[64,16]{1,0:T(8,128)S(1)} %copy-done.118, f32[64,1024]{1,0:T(8,128)S(1)} %copy-done.77, ...), kind=kLoop, calls=%fused_computation.32 | loop fusion | flops 31391744 | bytes 4030464 | tf_op jit(solution)/shard_map/reduce_sum | solution.py:47
  356.6 7.0 %multiply_reduce_fusion.21 = f32[64,1024]{1,0:T(8,128)} fusion(f32[64,16]{1,0:T(8,128)S(1)} %copy-done.101, f32[64,1024]{1,0:T(8,128)S(1)} %copy-done.65, f32[64,16]{1,0:T(8,128)S(1)} %copy-done.118, f32[64,1024]{1,0:T(8,128)S(1)} %copy-done.77, f32[16,1024]{1,0:T(8,128)S(1)} %exponential_negate_fusion, f32[64,1024]{1,0:T(8,128)S(1)} %copy-done.57, ...), kind=kLoop, calls=%fused_computation.34 | loop fusion | flops 27197440 | bytes 3502080 | tf_op jit(solution)/shard_map/reduce_sum | solution.py:47
  363.7 1.5 pad_maximum_fusion
  365.1 18.5 %pad.62 = f32[63,16,1024]{2,1,0:T(8,128)} pad(f32[32,16,1024]{2,1,0:T(8,128)} %pad_maximum_fusion, f32[]{:T(128)} %constant.4.clone.1), padding=0_0_1x0_0_0x0_0_0 | pad | bytes 6225924 | tf_op jit(solution)/shard_map/slice | solution.py:52
  383.6 12.1 %pad.86 = f32[64,16,1024]{2,1,0:T(8,128)} pad(f32[32,16,1024]{2,1,0:T(8,128)S(1)} %copy-done.10, f32[]{:T(128)} %constant.4.clone.1), padding=1_0_1x0_0_0x0_0_0 | pad | bytes 6291460
  395.8 4.4 slice_add_fusion.35
  400.4 9.3 %multiply_reduce_fusion.29 = (f32[64,1024]{1,0:T(8,128)S(1)}, f32[64,1024]{1,0:T(8,128)S(1)}, f32[64,1024]{1,0:T(8,128)S(1)}, f32[64,1024]{1,0:T(8,128)S(1)}, f32[64,1024]{1,0:T(8,128)S(1)}, /*index=5*/f32[64,1024]{1,0:T(8,128)S(1)}) fusion(f32[64,16]{1,0:T(8,128)S(1)} %copy-done.106, f32[64,1024]{1,0:T(8,128)S(1)} %copy-done.62, ...), kind=kLoop, calls=%fused_computation.42 | loop fusion | flops 27918336 | bytes 7630848 | tf_op jit(solution)/shard_map/reduce_sum | solution.py:47
  410.6 7.3 %multiply_reduce_fusion.23 = (f32[64,1024]{1,0:T(8,128)S(1)}, f32[64,1024]{1,0:T(8,128)S(1)}, f32[64,1024]{1,0:T(8,128)S(1)}) fusion(f32[64,16]{1,0:T(8,128)S(1)} %copy-done.103, f32[64,1024]{1,0:T(8,128)S(1)} %copy-done.58, f32[64,16]{1,0:T(8,128)S(1)} %copy-done.110, f32[64,1024]{1,0:T(8,128)S(1)} %copy-done.60, f32[64,16]{1,0:T(8,128)S(1)} %copy-done.112, ...), kind=kLoop, calls=%fused_computation.36 | loop fusion | flops 27066368 | bytes 3506176 | tf_op jit(solution)/shard_map/reduce_sum | solution.py:47
  418.1 9.0 %multiply_reduce_fusion = (f32[64,1024]{1,0:T(8,128)S(1)}, f32[64,1024]{1,0:T(8,128)S(1)}, f32[64,1024]{1,0:T(8,128)S(1)}, f32[64,1024]{1,0:T(8,128)S(1)}, f32[64,1024]{1,0:T(8,128)S(1)}, /*index=5*/f32[64,1024]{1,0:T(8,128)S(1)}) fusion(f32[64,16]{1,0:T(8,128)S(1)} %copy-done.100, f32[16,1024]{1,0:T(8,128)S(1)} %exponential_negate_fusion, ...), kind=kLoop, calls=%fused_computation.13 | loop fusion | flops 24772608 | bytes 7364608 | tf_op jit(solution)/shard_map/reduce_sum | solution.py:56
  427.1 0.7 add_dynamic-update-slice_fusion.14
  428.6 0.7 add_dynamic-update-slice_fusion.12
  429.4 0.7 add_dynamic-update-slice_fusion.11
  430.9 6.1 %multiply_reduce_fusion.9 = (f32[64,1024]{1,0:T(8,128)S(1)}, f32[64,1024]{1,0:T(8,128)S(1)}, f32[64,1024]{1,0:T(8,128)S(1)}, f32[64,1024]{1,0:T(8,128)S(1)}) fusion(f32[64,16]{1,0:T(8,128)S(1)} %copy-done.90, f32[64,1024]{1,0:T(8,128)S(1)} %copy-done.16, f32[64,16]{1,0:T(8,128)S(1)} %copy-done.86, f32[64,1024]{1,0:T(8,128)S(1)} %copy-done.26, ...), kind=kLoop, calls=%fused_computation.22 | loop fusion | flops 20709376 | bytes 6909952 | tf_op jit(solution)/shard_map/reduce_sum | solution.py:47
  437.2 9.0 %multiply_reduce_fusion.2 = (f32[64,1024]{1,0:T(8,128)S(1)}, f32[64,1024]{1,0:T(8,128)S(1)}, f32[64,1024]{1,0:T(8,128)S(1)}, f32[64,1024]{1,0:T(8,128)S(1)}, f32[64,1024]{1,0:T(8,128)S(1)}, /*index=5*/f32[64,1024]{1,0:T(8,128)S(1)}) fusion(f32[64,1024]{1,0:T(8,128)S(1)} %copy-done.33, f32[64,16]{1,0:T(8,128)S(1)} %copy-done.82, ...), kind=kLoop, calls=%fused_computation.15 | loop fusion | flops 24772608 | bytes 7364608 | tf_op jit(solution)/shard_map/reduce_sum | solution.py:56
  446.2 0.7 add_dynamic-update-slice_fusion.9
  447.0 0.7 add_dynamic-update-slice_fusion.8
  449.9 0.7 add_dynamic-update-slice_fusion.4
  451.4 0.8 add_dynamic-update-slice_fusion.2
  452.1 0.7 add_dynamic-update-slice_fusion.1
  452.9 0.7 add_dynamic-update-slice_fusion
  453.6 5.0 reshape.121
  458.7 9.1 %fusion.1 = bf16[1024,1024]{1,0:T(8,128)(2,1)S(1)} fusion(f32[1024,1024]{1,0:T(8,128)} %reshape.121, f32[1024]{0:T(1024)S(1)} %copy-done.122, f32[1024,1024]{1,0:T(8,128)} %bitcast.25, f32[1024]{0:T(1024)S(1)} %bitcast.36, f32[1024]{0:T(1024)S(1)} %bitcast.38, f32[1024]{0:T(1024)S(1)} %bitcast.34, f32[1024]{0:T(1024)S(1)} %bitcast.32, ...), kind=kLoop, calls=%fused_computation.7 | loop fusion | flops 17825792 | bytes 10510336 | tf_op jit(solution)/shard_map/convert_element_type | solution.py:97
  467.8 50.8 %all_to_all.26 = bf16[8,128,1024]{2,1,0:T(8,128)(2,1)S(1)} all-to-all(bf16[8,128,1024]{2,1,0:T(8,128)(2,1)S(1)} %bitcast.29), channel_id=1, replica_groups=mesh['seq'=8,'batch'=4] {'seq'}, dimensions={0} | all-to-all | bytes 4194304 | tf_op jit(solution)/shard_map/all_to_all | solution.py:98
  519.4 1.3 copy-done.14
  520.7 2.5 fusion.8
  (287 shorter events, 14.1 us)
Async XLA Ops:
  6.5 64.4 %copy-start = (bf16[1024,288]{0,1:T(8,128)(2,1)S(1)}, bf16[1024,288]{0,1:T(8,128)(2,1)}, u32[]{:S(2)}) copy-start(bf16[1024,288]{0,1:T(8,128)(2,1)} %param.14) | copy-start | bytes 1769476
  6.5 10.6 %copy-start.123 = (bf16[1024]{0:T(1024)(128)(2,1)S(1)}, bf16[1024]{0:T(1024)(128)(2,1)}, u32[]{:S(2)}) copy-start(bf16[1024]{0:T(1024)(128)(2,1)} %param.13) | copy-start | bytes 6148
  6.5 10.6 %copy-start.121 = (bf16[4,1024]{1,0:T(4,128)(2,1)S(1)}, bf16[4,1024]{1,0:T(4,128)(2,1)}, u32[]{:S(2)}) copy-start(bf16[4,1024]{1,0:T(4,128)(2,1)} %param.12) | copy-start | bytes 24580
  9.8 55.5 %all-to-all-start = ((bf16[128,8,1024]{2,0,1:T(8,128)(2,1)}), bf16[128,8,1024]{2,0,1:T(8,128)(2,1)S(1)}, u32[]{:S(2)}, u32[]{:S(2)}) async-start(bf16[128,8,1024]{2,0,1:T(8,128)(2,1)} %bitcast.28), calls=%async_computation | async-start | bytes 4194304 | tf_op jit(solution)/shard_map/all_to_all | solution.py:78
  17.1 192.2 %all-gather.3.cloned.1.call-start = ((), (), s32[]{:S(2)}) async-start(), calls=%async_computation.2 | async-start | bytes 10616832 | tf_op jit(solution)/shard_map/all_gather | solution.py:8
  17.2 48.6 %copy-start.94 = (f32[1,1024]{1,0:T(1,128)}, f32[1,1024]{1,0:T(1,128)S(1)}, u32[]{:S(2)}) copy-start(f32[1,1024]{1,0:T(1,128)S(1)} %get-tuple-element.141) | copy-start | bytes 12292
  239.0 13.8 %copy-start.21 = (f32[64,1024]{1,0:T(8,128)}, f32[64,1024]{1,0:T(8,128)S(1)}, u32[]{:S(2)}) copy-start(f32[64,1024]{1,0:T(8,128)S(1)} %get-tuple-element.66) | copy-start | bytes 786436
  239.0 13.8 %copy-start.23 = (f32[64,1024]{1,0:T(8,128)}, f32[64,1024]{1,0:T(8,128)S(1)}, u32[]{:S(2)}) copy-start(f32[64,1024]{1,0:T(8,128)S(1)} %get-tuple-element.67) | copy-start | bytes 786436
  239.0 13.8 %copy-start.25 = (f32[64,1024]{1,0:T(8,128)}, f32[64,1024]{1,0:T(8,128)S(1)}, u32[]{:S(2)}) copy-start(f32[64,1024]{1,0:T(8,128)S(1)} %get-tuple-element.68) | copy-start | bytes 786436
  241.2 11.7 %copy-start.45 = (f32[64,1024]{1,0:T(8,128)}, f32[64,1024]{1,0:T(8,128)S(1)}, u32[]{:S(2)}) copy-start(f32[64,1024]{1,0:T(8,128)S(1)} %get-tuple-element.58) | copy-start | bytes 786436
  241.2 11.7 %copy-start.47 = (f32[64,1024]{1,0:T(8,128)}, f32[64,1024]{1,0:T(8,128)S(1)}, u32[]{:S(2)}) copy-start(f32[64,1024]{1,0:T(8,128)S(1)} %get-tuple-element.59) | copy-start | bytes 786436
  241.2 11.7 %copy-start.49 = (f32[64,1024]{1,0:T(8,128)}, f32[64,1024]{1,0:T(8,128)S(1)}, u32[]{:S(2)}) copy-start(f32[64,1024]{1,0:T(8,128)S(1)} %get-tuple-element.60) | copy-start | bytes 786436
  241.2 35.4 %copy-start.29 = (f32[64,1024]{1,0:T(8,128)}, f32[64,1024]{1,0:T(8,128)S(1)}, u32[]{:S(2)}) copy-start(f32[64,1024]{1,0:T(8,128)S(1)} %get-tuple-element.41) | copy-start | bytes 786436
  244.0 32.6 %copy-start.81 = (f32[64,16]{1,0:T(8,128)}, f32[64,16]{1,0:T(8,128)S(1)}, u32[]{:S(2)}) copy-start(f32[64,16]{1,0:T(8,128)S(1)} %get-tuple-element.108) | copy-start | bytes 12292
  252.8 23.1 %copy-start.15 = (f32[64,1024]{1,0:T(8,128)}, f32[64,1024]{1,0:T(8,128)S(1)}, u32[]{:S(2)}) copy-start(f32[64,1024]{1,0:T(8,128)S(1)} %get-tuple-element.79) | copy-start | bytes 786436
  252.8 23.1 %copy-start.17 = (f32[64,1024]{1,0:T(8,128)}, f32[64,1024]{1,0:T(8,128)S(1)}, u32[]{:S(2)}) copy-start(f32[64,1024]{1,0:T(8,128)S(1)} %get-tuple-element.80) | copy-start | bytes 786436
  252.8 23.1 %copy-start.19 = (f32[64,1024]{1,0:T(8,128)}, f32[64,1024]{1,0:T(8,128)S(1)}, u32[]{:S(2)}) copy-start(f32[64,1024]{1,0:T(8,128)S(1)} %get-tuple-element.81) | copy-start | bytes 786436
  252.8 23.1 %copy-start.54 = (f32[64,1024]{1,0:T(8,128)}, f32[64,1024]{1,0:T(8,128)S(1)}, u32[]{:S(2)}) copy-start(f32[64,1024]{1,0:T(8,128)S(1)} %get-tuple-element.74) | copy-start | bytes 786436
  275.9 8.5 %copy-start.7 = (f32[64,16,1024]{2,1,0:T(8,128)}, f32[64,16,1024]{2,1,0:T(8,128)S(1)}, u32[]{:S(2)}) copy-start(f32[64,16,1024]{2,1,0:T(8,128)S(1)} %get-tuple-element.38) | copy-start | bytes 12582916
  290.6 10.7 %copy-start.72 = (f32[1,16,1024]{2,1,0:T(8,128)S(1)}, f32[1,16,1024]{2,1,0:T(8,128)}, u32[]{:S(2)}) copy-start(f32[1,16,1024]{2,1,0:T(8,128)} %slice.548) | copy-start | bytes 196612
  339.3 9.1 %copy-start.98 = (f32[64,16]{1,0:T(8,128)S(1)}, f32[64,16]{1,0:T(8,128)}, u32[]{:S(2)}) copy-start(f32[64,16]{1,0:T(8,128)} %get-tuple-element.115) | copy-start | bytes 12292
  348.5 8.2 %copy-start.101 = (f32[64,16]{1,0:T(8,128)S(1)}, f32[64,16]{1,0:T(8,128)}, u32[]{:S(2)}) copy-start(f32[64,16]{1,0:T(8,128)} %get-tuple-element.116) | copy-start | bytes 12292
  363.7 19.9 %copy-start.10 = (f32[32,16,1024]{2,1,0:T(8,128)S(1)}, f32[32,16,1024]{2,1,0:T(8,128)}, u32[]{:S(2)}) copy-start(f32[32,16,1024]{2,1,0:T(8,128)} %add.327) | copy-start | bytes 6291460
  400.3 10.1 %copy-start.56 = (f32[64,1024]{1,0:T(8,128)S(1)}, f32[64,1024]{1,0:T(8,128)}, u32[]{:S(2)}) copy-start(f32[64,1024]{1,0:T(8,128)} %copy-done.54) | copy-start | bytes 786436
  400.3 10.1 %copy-start.58 = (f32[64,1024]{1,0:T(8,128)S(1)}, f32[64,1024]{1,0:T(8,128)}, u32[]{:S(2)}) copy-start(f32[64,1024]{1,0:T(8,128)} %get-tuple-element.86) | copy-start | bytes 786436
  400.3 10.1 %copy-start.60 = (f32[64,1024]{1,0:T(8,128)S(1)}, f32[64,1024]{1,0:T(8,128)}, u32[]{:S(2)}) copy-start(f32[64,1024]{1,0:T(8,128)} %get-tuple-element.87) | copy-start | bytes 786436
  400.4 10.1 %copy-start.74 = (f32[64,1024]{1,0:T(8,128)S(1)}, f32[64,1024]{1,0:T(8,128)}, u32[]{:S(2)}) copy-start(f32[64,1024]{1,0:T(8,128)} %get-tuple-element.62) | copy-start | bytes 786436
  400.4 10.1 %copy-start.103 = (f32[64,16]{1,0:T(8,128)S(1)}, f32[64,16]{1,0:T(8,128)}, u32[]{:S(2)}) copy-start(f32[64,16]{1,0:T(8,128)} %get-tuple-element.117) | copy-start | bytes 12292
  400.4 10.1 %copy-start.104 = (f32[64,16]{1,0:T(8,128)S(1)}, f32[64,16]{1,0:T(8,128)}, u32[]{:S(2)}) copy-start(f32[64,16]{1,0:T(8,128)} %get-tuple-element.118) | copy-start | bytes 12292
  400.4 10.1 %copy-start.105 = (f32[64,16]{1,0:T(8,128)S(1)}, f32[64,16]{1,0:T(8,128)}, u32[]{:S(2)}) copy-start(f32[64,16]{1,0:T(8,128)} %get-tuple-element.119) | copy-start | bytes 12292
  400.4 10.1 %copy-start.108 = (f32[64,16]{1,0:T(8,128)S(1)}, f32[64,16]{1,0:T(8,128)}, u32[]{:S(2)}) copy-start(f32[64,16]{1,0:T(8,128)} %get-tuple-element.122) | copy-start | bytes 12292
  400.4 10.1 %copy-start.110 = (f32[64,16]{1,0:T(8,128)S(1)}, f32[64,16]{1,0:T(8,128)}, u32[]{:S(2)}) copy-start(f32[64,16]{1,0:T(8,128)} %get-tuple-element.134) | copy-start | bytes 12292
  400.4 10.1 %copy-start.112 = (f32[64,16]{1,0:T(8,128)S(1)}, f32[64,16]{1,0:T(8,128)}, u32[]{:S(2)}) copy-start(f32[64,16]{1,0:T(8,128)} %get-tuple-element.135) | copy-start | bytes 12292
  410.5 7.4 %copy-start.30 = (f32[64,1024]{1,0:T(8,128)S(1)}, f32[64,1024]{1,0:T(8,128)}, u32[]{:S(2)}) copy-start(f32[64,1024]{1,0:T(8,128)} %copy-done.29) | copy-start | bytes 786436
  410.5 7.4 %copy-start.40 = (f32[64,1024]{1,0:T(8,128)S(1)}, f32[64,1024]{1,0:T(8,128)}, u32[]{:S(2)}) copy-start(f32[64,1024]{1,0:T(8,128)} %get-tuple-element.51) | copy-start | bytes 786436
  410.6 7.4 %copy-start.41 = (f32[64,1024]{1,0:T(8,128)S(1)}, f32[64,1024]{1,0:T(8,128)}, u32[]{:S(2)}) copy-start(f32[64,1024]{1,0:T(8,128)} %get-tuple-element.52) | copy-start | bytes 786436
  410.6 7.4 %copy-start.42 = (f32[64,1024]{1,0:T(8,128)S(1)}, f32[64,1024]{1,0:T(8,128)}, u32[]{:S(2)}) copy-start(f32[64,1024]{1,0:T(8,128)} %get-tuple-element.53) | copy-start | bytes 786436
  410.6 7.4 %copy-start.43 = (f32[64,1024]{1,0:T(8,128)S(1)}, f32[64,1024]{1,0:T(8,128)}, u32[]{:S(2)}) copy-start(f32[64,1024]{1,0:T(8,128)} %get-tuple-element.54) | copy-start | bytes 786436
  410.6 7.4 %copy-start.44 = (f32[64,1024]{1,0:T(8,128)S(1)}, f32[64,1024]{1,0:T(8,128)}, u32[]{:S(2)}) copy-start(f32[64,1024]{1,0:T(8,128)} %get-tuple-element.55) | copy-start | bytes 786436
  418.0 12.1 %copy-start.70 = (f32[64,1024]{1,0:T(8,128)S(1)}, f32[64,1024]{1,0:T(8,128)}, u32[]{:S(2)}) copy-start(f32[64,1024]{1,0:T(8,128)} %multiply_reduce_fusion.21) | copy-start | bytes 786436
  418.0 12.9 %copy-start.13 = (f32[64,16,1024]{2,1,0:T(8,128)S(1)}, f32[64,16,1024]{2,1,0:T(8,128)}, u32[]{:S(2)}) copy-start(f32[64,16,1024]{2,1,0:T(8,128)} %get-tuple-element.40) | copy-start | bytes 12582916
  418.0 12.8 %copy-start.16 = (f32[64,1024]{1,0:T(8,128)S(1)}, f32[64,1024]{1,0:T(8,128)}, u32[]{:S(2)}) copy-start(f32[64,1024]{1,0:T(8,128)} %copy-done.15) | copy-start | bytes 786436
  418.0 12.8 %copy-start.18 = (f32[64,1024]{1,0:T(8,128)S(1)}, f32[64,1024]{1,0:T(8,128)}, u32[]{:S(2)}) copy-start(f32[64,1024]{1,0:T(8,128)} %copy-done.17) | copy-start | bytes 786436
  418.0 12.8 %copy-start.20 = (f32[64,1024]{1,0:T(8,128)S(1)}, f32[64,1024]{1,0:T(8,128)}, u32[]{:S(2)}) copy-start(f32[64,1024]{1,0:T(8,128)} %copy-done.19) | copy-start | bytes 786436
  418.0 12.8 %copy-start.22 = (f32[64,1024]{1,0:T(8,128)S(1)}, f32[64,1024]{1,0:T(8,128)}, u32[]{:S(2)}) copy-start(f32[64,1024]{1,0:T(8,128)} %copy-done.21) | copy-start | bytes 786436
  418.0 12.8 %copy-start.24 = (f32[64,1024]{1,0:T(8,128)S(1)}, f32[64,1024]{1,0:T(8,128)}, u32[]{:S(2)}) copy-start(f32[64,1024]{1,0:T(8,128)} %copy-done.23) | copy-start | bytes 786436
  418.1 12.8 %copy-start.26 = (f32[64,1024]{1,0:T(8,128)S(1)}, f32[64,1024]{1,0:T(8,128)}, u32[]{:S(2)}) copy-start(f32[64,1024]{1,0:T(8,128)} %copy-done.25) | copy-start | bytes 786436
  418.1 12.8 %copy-start.80 = (f32[64,16]{1,0:T(8,128)S(1)}, f32[64,16]{1,0:T(8,128)}, u32[]{:S(2)}) copy-start(f32[64,16]{1,0:T(8,128)} %get-tuple-element.106) | copy-start | bytes 12292
  418.1 12.8 %copy-start.83 = (f32[64,16]{1,0:T(8,128)S(1)}, f32[64,16]{1,0:T(8,128)}, u32[]{:S(2)}) copy-start(f32[64,16]{1,0:T(8,128)} %get-tuple-element.112) | copy-start | bytes 12292
  418.1 12.8 %copy-start.84 = (f32[64,16]{1,0:T(8,128)S(1)}, f32[64,16]{1,0:T(8,128)}, u32[]{:S(2)}) copy-start(f32[64,16]{1,0:T(8,128)} %get-tuple-element.113) | copy-start | bytes 12292
  418.1 12.8 %copy-start.86 = (f32[64,16]{1,0:T(8,128)S(1)}, f32[64,16]{1,0:T(8,128)}, u32[]{:S(2)}) copy-start(f32[64,16]{1,0:T(8,128)} %get-tuple-element.127) | copy-start | bytes 12292
  418.1 12.8 %copy-start.88 = (f32[64,16]{1,0:T(8,128)S(1)}, f32[64,16]{1,0:T(8,128)}, u32[]{:S(2)}) copy-start(f32[64,16]{1,0:T(8,128)} %get-tuple-element.128) | copy-start | bytes 12292
  418.1 12.8 %copy-start.89 = (f32[64,16]{1,0:T(8,128)S(1)}, f32[64,16]{1,0:T(8,128)}, u32[]{:S(2)}) copy-start(f32[64,16]{1,0:T(8,128)} %get-tuple-element.129) | copy-start | bytes 12292
  429.3 7.8 %copy-start.33 = (f32[64,1024]{1,0:T(8,128)S(1)}, f32[64,1024]{1,0:T(8,128)}, u32[]{:S(2)}) copy-start(f32[64,1024]{1,0:T(8,128)} %get-tuple-element.42) | copy-start | bytes 786436
  429.3 7.8 %copy-start.34 = (f32[64,1024]{1,0:T(8,128)S(1)}, f32[64,1024]{1,0:T(8,128)}, u32[]{:S(2)}) copy-start(f32[64,1024]{1,0:T(8,128)} %get-tuple-element.46) | copy-start | bytes 786436
  429.3 7.8 %copy-start.35 = (f32[64,1024]{1,0:T(8,128)S(1)}, f32[64,1024]{1,0:T(8,128)}, u32[]{:S(2)}) copy-start(f32[64,1024]{1,0:T(8,128)} %get-tuple-element.47) | copy-start | bytes 786436
  429.3 7.8 %copy-start.36 = (f32[64,1024]{1,0:T(8,128)S(1)}, f32[64,1024]{1,0:T(8,128)}, u32[]{:S(2)}) copy-start(f32[64,1024]{1,0:T(8,128)} %get-tuple-element.48) | copy-start | bytes 786436
  429.3 7.8 %copy-start.37 = (f32[64,1024]{1,0:T(8,128)S(1)}, f32[64,1024]{1,0:T(8,128)}, u32[]{:S(2)}) copy-start(f32[64,1024]{1,0:T(8,128)} %get-tuple-element.49) | copy-start | bytes 786436
  429.3 7.8 %copy-start.38 = (f32[64,1024]{1,0:T(8,128)S(1)}, f32[64,1024]{1,0:T(8,128)}, u32[]{:S(2)}) copy-start(f32[64,1024]{1,0:T(8,128)} %get-tuple-element.50) | copy-start | bytes 786436
  429.4 7.8 %copy-start.82 = (f32[64,16]{1,0:T(8,128)S(1)}, f32[64,16]{1,0:T(8,128)}, u32[]{:S(2)}) copy-start(f32[64,16]{1,0:T(8,128)} %copy-done.81) | copy-start | bytes 12292
  429.4 7.8 %copy-start.97 = (f32[64,16]{1,0:T(8,128)S(1)}, f32[64,16]{1,0:T(8,128)}, u32[]{:S(2)}) copy-start(f32[64,16]{1,0:T(8,128)} %get-tuple-element.114) | copy-start | bytes 12292
  429.4 7.8 %copy-start.99 = (f32[64,16]{1,0:T(8,128)S(1)}, f32[64,16]{1,0:T(8,128)}, u32[]{:S(2)}) copy-start(f32[64,16]{1,0:T(8,128)} %get-tuple-element.115) | copy-start | bytes 12292
  437.2 9.1 %copy-start.69 = (f32[64,1024]{1,0:T(8,128)S(1)}, f32[64,1024]{1,0:T(8,128)}, u32[]{:S(2)}) copy-start(f32[64,1024]{1,0:T(8,128)} %multiply_reduce_fusion.19) | copy-start | bytes 786436
  437.2 9.8 %copy-start.66 = (f32[64,1024]{1,0:T(8,128)S(1)}, f32[64,1024]{1,0:T(8,128)}, u32[]{:S(2)}) copy-start(f32[64,1024]{1,0:T(8,128)} %multiply_reduce_fusion.17) | copy-start | bytes 786436
  (65 other events, 219.9 us)
Sparse Core Ops, SparseCore 0:
  73.0 136.2 all-gather.2
